TPU v7x, 32 devices: a whole 2x2x4 slice. The times are simulated.
32 devices in a mesh: row: 2 (over x), col: 16 (over z, y, core).
Axes of the slice: x: 2, y: 2, z: 4, core: 2. Of those that a mesh axis runs over, the one named last changes fastest.
Arguments:
- ld_matrix: bfloat16 [32768, 32768], P('row', 'col'), may hold values from -0.23925781 to 0.23925781
- factor: float32 [32768, 256], P(('row', 'col')), may hold values from -0.24 to 0.24
- diag_values: bfloat16 [32768], P('col'), may hold values from 0.5 to 4
Outputs:
- factor_grad: float32 [32768, 256], P(('row', 'col'))
All inputs are finite; a program needn't handle non-finite values.
Results may differ from a plain program's by a relative error of at most 0.003.
Values may be sent and summed in bfloat16 or wider, within the bound.
A program may use at most 128 MiB of HBM per device.

v0:
```python
import math
import jax
import jax.numpy as jnp
from jax import lax
from jax.sharding import PartitionSpec as P


def from_root(value, axis, source):
    kept = jnp.where(lax.axis_index(axis) == source, value, 0).astype(value.dtype)
    return lax.psum(kept, axis)


def local(ld_matrix, factor, diag_values):
    factor_low = factor.astype(jnp.bfloat16)
    row_height = ld_matrix.shape[0]
    col_width = ld_matrix.shape[1]
    rank_width = factor.shape[1]
    row_panel = lax.all_gather(factor_low, "col", axis=0, tiled=True)
    col_index = lax.axis_index("col")
    row_index = lax.axis_index("row")
    per_row = lax.axis_size("col") // lax.axis_size("row")
    offset = col_index % per_row * col_width
    section = lax.dynamic_slice_in_dim(row_panel, offset, col_width, 0)
    col_panel = from_root(section, "row", col_index // per_row)
    diag_float = diag_values.astype(jnp.float32)
    col_ids = col_index * col_width + jnp.arange(col_width, dtype=jnp.int32)
    own_rows = row_height // lax.axis_size("col")
    height = math.gcd(own_rows * lax.axis_size("col"), 512)
    number = own_rows * lax.axis_size("col") // height

    def one_block(number_index):
        first = number_index * height
        ld_block = lax.dynamic_slice_in_dim(ld_matrix, first, height, 0)
        left = lax.dynamic_slice_in_dim(row_panel, first, height, 0)
        row_ids = row_index * row_height + first + jnp.arange(height, dtype=jnp.int32)
        model_part = jnp.dot(left, col_panel.T, preferred_element_type=jnp.float32)
        ondiag = row_ids[:, None] == col_ids[None, :]
        extra = jnp.where(ondiag, diag_float[None, :], jnp.float32(0.0))
        misfit = (model_part + extra - ld_block.astype(jnp.float32)).astype(jnp.bfloat16)
        return 4.0 * jnp.dot(misfit, col_panel, preferred_element_type=jnp.float32)

    blocks = lax.map(one_block, jnp.arange(number, dtype=jnp.int32))
    return lax.psum_scatter(
        blocks.reshape(own_rows * lax.axis_size("col"), rank_width),
        "col",
        scatter_dimension=0,
        tiled=True,
    )


def solution(mesh):
    in_specs = (P("row", "col"), P(("row", "col"), None), P("col"))
    out_specs = P(("row", "col"), None)
    return jax.shard_map(local, mesh=mesh, in_specs=in_specs, out_specs=out_specs, check_vma=False)
```

profile of v0, /device:TPU:0, one launch (start us, length us, event | category | flops | bytes accessed | tf_op | source)
XLA Modules:
  0.0 495.8 jit_solution(5465250970531595996)
XLA Ops:
  6.5 2.1 convert_element_type.18
  8.7 77.8 %all-gather.2.cloned.1.call-done = bf16[16384,256]{1,0:T(8,128)(2,1)} async-done(((bf16[1024,256]{1,0:T(8,128)(2,1)}), bf16[16384,256]{1,0:T(8,128)(2,1)}) %all-gather.2.cloned.1.call-update) | async-done | bytes 8388624 | tf_op jit(solution)/shard_map/all_gather | solution.py:18
  86.5 2.4 dynamic-slice_select_fusion
  89.0 0.7 convert_element_type.19
  89.7 38.1 %all-reduce.2.cloned.1.call-done = bf16[2048,256]{1,0:T(8,128)(2,1)} async-done(((bf16[2048,256]{1,0:T(8,128)(2,1)}), bf16[2048,256]{1,0:T(8,128)(2,1)}) %all-reduce.2.cloned.1.call-update) | async-done | bytes 1048592 | tf_op jit(solution)/shard_map/psum | solution.py:10
  127.8 183.9 %while.13 = (s32[]{:T(128)}, f32[32,512,256]{2,1,0:T(8,128)}, s32[32]{0:T(128)S(1)}, bf16[16384,256]{1,0:T(8,128)(2,1)}, bf16[2048,256]{1,0:T(8,128)(2,1)}, /*in...) while((s32[]{:T(128)}, f32[32,512,256]{2,1,0:T(8,128)}, ...), condition=%wide.region_2.3_spmd.clone, body=%wide.region_1.2_spmd.clone.sunk | while | flops 1080166912 | bytes 5011147 | solution.py:42
  127.8 0.6 dynamic_slice.35
  129.1 4.5 fusion.18
  133.5 0.6 dynamic_slice.35
  134.8 4.5 fusion.18
  140.6 4.5 fusion.18
  146.3 4.4 fusion.18
  152.0 4.5 fusion.18
  157.7 4.5 fusion.18
  162.2 0.6 dynamic_slice.35
  163.5 4.4 fusion.18
  167.9 0.6 dynamic_slice.35
  169.2 4.6 fusion.18
  175.0 4.5 fusion.18
  179.5 0.6 dynamic_slice.35
  180.8 4.5 fusion.18
  186.6 4.5 fusion.18
  191.1 0.6 dynamic_slice.35
  192.3 4.5 fusion.18
  198.1 4.5 fusion.18
  203.8 4.5 fusion.18
  209.5 4.5 fusion.18
  214.0 0.6 dynamic_slice.35
  215.3 4.6 fusion.18
  221.2 4.6 fusion.18
  227.0 4.5 fusion.18
  231.5 0.6 dynamic_slice.35
  232.8 4.4 fusion.18
  238.5 4.5 fusion.18
  244.2 4.5 fusion.18
  249.9 4.5 fusion.18
  255.7 4.4 fusion.18
  261.4 4.4 fusion.18
  267.1 4.5 fusion.18
  272.9 4.5 fusion.18
  277.4 0.6 dynamic_slice.35
  278.6 4.4 fusion.18
  284.3 4.4 fusion.18
  290.1 4.5 fusion.18
  295.8 4.5 fusion.18
  301.5 4.5 fusion.18
  307.3 4.5 fusion.18
  311.8 177.5 %reduce-scatter.2.cloned.1.call-done = f32[1024,256]{1,0:T(8,128)} async-done(((f32[16384,256]{1,0:T(8,128)}), f32[1024,256]{1,0:T(8,128)}) %reduce-scatter.2.cloned.1.call-update) | async-done | bytes 1048592 | tf_op jit(solution)/shard_map/reduce_scatter | solution.py:43
  (95 shorter events, 13.9 us)
Async XLA Ops:
  6.5 80.0 %all-gather.2.cloned.1.call-start = ((), (), s32[]{:S(2)}) async-start(), calls=%async_computation.1 | async-start | bytes 8912896 | tf_op jit(solution)/shard_map/all_gather | solution.py:18
  8.6 119.2 %all-reduce.2.cloned.1.call-start = ((), (), s32[]{:S(2)}) async-start(), calls=%async_computation.2 | async-start | bytes 2097152 | tf_op jit(solution)/shard_map/psum | solution.py:10
  88.9 400.3 %reduce-scatter.2.cloned.1.call-start = ((), (), s32[]{:S(2)}) async-start(), calls=%async_computation.3 | async-start | bytes 17825792 | tf_op jit(solution)/shard_map/reduce_scatter | solution.py:43
Sparse Core Ops, SparseCore 0:
  9.5 77.0 all-gather.1
  89.1 38.6 all-reduce.1
  311.9 177.3 reduce-scatter.1
where the time goes:
time: 496 us
  waiting for transfers between devices  293 us (59%)
  matrix products  143 us (29%)
  loops' own time  21.6 us (4%)
  local copies, waits for them, and re-layouts  18.6 us (4%)
  between operations  13.1 us (3%)
  other arithmetic  5.51 us (1%)
    reduce_scatter x1, waiting for transfers between devices, local(): lax.psum_scatter(blocks.reshape(own_rows * lax.axis_size('col'), rank_wid...  178 us
    dot_general x32, matrix products, one_block(): return 4.0 * jnp.dot(misfit, col_panel, preferred_element_type=jnp.float32)  143 us
    all_gather x1, waiting for transfers between devices, local(): row_panel = lax.all_gather(factor_low, 'col', axis=0, tiled=True)  77.8 us
    psum x1, waiting for transfers between devices, from_root(): return lax.psum(kept, axis)  38.1 us
    another operation x1, loops' own time, local(): blocks = lax.map(one_block, jnp.arange(number, dtype=jnp.int32))  21.6 us
    dynamic_slice x32, local copies, waits for them, and re-layouts, local(): blocks = lax.map(one_block, jnp.arange(number, dtype=jnp.int32))  18.6 us
  transfers between devices with their start and end apart: 3, of which 3 were waited for; matrix products, arithmetic and copies ran while one was open for 0% of the time, Pallas kernels for 0%

commit v1 on v0

--- a/solution.py
+++ b/solution.py
@@ -7,7 +7,7 @@
 
 def from_root(value, axis, source):
     kept = jnp.where(lax.axis_index(axis) == source, value, 0).astype(value.dtype)
-    return lax.psum(kept, axis)
+    return jnp.sum(lax.all_gather(kept, axis), axis=0)
 
 
 def local(ld_matrix, factor, diag_values):

time: 496 us -> 475 us (0.958)
  matrix products: 143 us -> 125 us
  waiting for transfers between devices: 293 us -> 286 us
    psum x1 -> x0, waiting for transfers between devices: 38.1 us -> none  [from_root(): return lax.psum(kept, axis)]
    all_gather x0 -> x1, waiting for transfers between devices: none -> 31.1 us  [from_root(): return jnp.sum(lax.all_gather(kept, axis), axis=0)]
    dot_general x32, matrix products: 143 us -> 125 us  [one_block(): return 4.0 * jnp.dot(misfit, col_panel, preferred_element_type=jnp.float32)]
where the time goes in v1:
time: 475 us; the launch traced here: 473 us
  waiting for transfers between devices  286 us (60%)
  matrix products  125 us (26%)
  loops' own time  21.6 us (5%)
  local copies, waits for them, and re-layouts  18.6 us (4%)
  between operations  13.2 us (3%)
  other arithmetic  8.15 us (2%)
    reduce_scatter x1, waiting for transfers between devices, local(): lax.psum_scatter(blocks.reshape(own_rows * lax.axis_size('col'), rank_wid...  178 us
    dot_general x32, matrix products, one_block(): return 4.0 * jnp.dot(misfit, col_panel, preferred_element_type=jnp.float32)  125 us
    all_gather x1, waiting for transfers between devices, local(): row_panel = lax.all_gather(factor_low, 'col', axis=0, tiled=True)  77.8 us
    all_gather x1, waiting for transfers between devices, from_root(): return jnp.sum(lax.all_gather(kept, axis), axis=0)  31.1 us
    another operation x1, loops' own time, local(): blocks = lax.map(one_block, jnp.arange(number, dtype=jnp.int32))  21.6 us
    dynamic_slice x32, local copies, waits for them, and re-layouts, local(): blocks = lax.map(one_block, jnp.arange(number, dtype=jnp.int32))  18.6 us
  transfers between devices with their start and end apart: 3, of which 3 were waited for; matrix products, arithmetic and copies ran while one was open for 0% of the time, Pallas kernels for 0%

profile of v1, /device:TPU:0, one launch (start us, length us, event | category | flops | bytes accessed | tf_op | source)
XLA Modules:
  0.0 473.0 jit_solution(5241089670545290282)
XLA Ops:
  6.5 2.1 convert_element_type.20
  8.7 77.8 %all-gather.4.cloned.1.call-done = bf16[16384,256]{1,0:T(8,128)(2,1)} async-done(((bf16[1024,256]{1,0:T(8,128)(2,1)}), bf16[16384,256]{1,0:T(8,128)(2,1)}) %all-gather.4.cloned.1.call-update) | async-done | bytes 8388624 | tf_op jit(solution)/shard_map/all_gather | solution.py:18
  86.5 2.4 dynamic-slice_select_fusion
  89.0 0.7 convert_element_type.21
  89.7 31.1 %all-gather.6.cloned.1.call-done = bf16[4096,256]{1,0:T(8,128)(2,1)} async-done(((bf16[2048,256]{1,0:T(8,128)(2,1)}), bf16[4096,256]{1,0:T(8,128)(2,1)}) %all-gather.6.cloned.1.call-update) | async-done | bytes 2097168 | tf_op jit(solution)/shard_map/all_gather | solution.py:10
  120.8 2.6 reduce_sum.12
  123.4 165.5 %while.13 = (s32[]{:T(128)}, f32[32,512,256]{2,1,0:T(8,128)}, s32[32]{0:T(128)S(1)}, bf16[16384,256]{1,0:T(8,128)(2,1)}, bf16[2048,256]{1,0:T(8,128)(2,1)S(1)}, ...) while((s32[]{:T(128)}, f32[32,512,256]{2,1,0:T(8,128)}, ...), condition=%wide.region_2.3_spmd.clone, body=%wide.region_1.2_spmd.clone.sunk | while | flops 1080166912 | bytes 5011147 | solution.py:42
  123.4 0.6 dynamic_slice.35
  124.7 3.9 fusion.18
  129.9 3.9 fusion.18
  135.0 3.9 fusion.18
  140.2 3.9 fusion.18
  145.4 3.9 fusion.18
  150.5 3.9 fusion.18
  154.4 0.6 dynamic_slice.35
  155.7 3.9 fusion.18
  160.9 3.9 fusion.18
  166.0 3.9 fusion.18
  171.2 3.9 fusion.18
  175.1 0.6 dynamic_slice.35
  176.4 3.9 fusion.18
  181.6 3.9 fusion.18
  186.7 3.9 fusion.18
  191.9 3.9 fusion.18
  195.8 0.6 dynamic_slice.35
  197.1 3.9 fusion.18
  202.2 3.9 fusion.18
  207.4 3.9 fusion.18
  212.6 3.9 fusion.18
  216.6 0.6 dynamic_slice.35
  217.8 3.9 fusion.18
  223.0 3.9 fusion.18
  228.1 3.9 fusion.18
  232.0 0.6 dynamic_slice.35
  233.3 3.9 fusion.18
  237.2 0.6 dynamic_slice.35
  238.5 3.9 fusion.18
  242.4 0.6 dynamic_slice.35
  243.6 3.9 fusion.18
  248.8 3.9 fusion.18
  254.0 3.9 fusion.18
  259.2 3.9 fusion.18
  264.3 3.9 fusion.18
  269.5 3.9 fusion.18
  274.7 3.9 fusion.18
  279.8 3.9 fusion.18
  285.0 3.9 fusion.18
  288.9 177.5 %reduce-scatter.2.cloned.1.call-done = f32[1024,256]{1,0:T(8,128)} async-done(((f32[16384,256]{1,0:T(8,128)}), f32[1024,256]{1,0:T(8,128)}) %reduce-scatter.2.cloned.1.call-update) | async-done | bytes 1048592 | tf_op jit(solution)/shard_map/reduce_scatter | solution.py:43
  (96 shorter events, 14.5 us)
Async XLA Ops:
  6.5 80.0 %all-gather.4.cloned.1.call-start = ((), (), s32[]{:S(2)}) async-start(), calls=%async_computation.1 | async-start | bytes 8912896 | tf_op jit(solution)/shard_map/all_gather | solution.py:18
  8.6 112.1 %all-gather.6.cloned.1.call-start = ((), (), s32[]{:S(2)}) async-start(), calls=%async_computation.3 | async-start | bytes 3145728 | tf_op jit(solution)/shard_map/all_gather | solution.py:10
  88.9 377.5 %reduce-scatter.2.cloned.1.call-start = ((), (), s32[]{:S(2)}) async-start(), calls=%async_computation.2 | async-start | bytes 17825792 | tf_op jit(solution)/shard_map/reduce_scatter | solution.py:43
Sparse Core Ops, SparseCore 0:
  9.5 77.0 all-gather.3
  89.1 31.6 all-gather.5
  289.1 177.3 reduce-scatter.1
